TPU v7x, 32 devices: a whole 2x2x4 slice. The times are simulated.
32 devices in a mesh: row: 8 (over y, x, core), col: 4 (over z).
Axes of the slice: x: 2, y: 2, z: 4, core: 2. Of those that a mesh axis runs over, the one named last changes fastest.
Arguments:
- observed: float32 [1024, 2048], P('row', 'col'), may hold values from -6 to 6
- psf_table: bfloat16 [64, 31, 31], replicated, may hold values from 0.049804688 to 1
- psf_index: int32 [8, 16], P('row', 'col'), may hold values from 0 to 63
- start_image: float32 [1024, 2048], P('row', 'col'), may hold values from -6 to 6
- blur_dual: float32 [1024, 2048], P('row', 'col'), may hold values from -6 to 6
- tv_dual: float32 [2, 1024, 2048], P(None, 'row', 'col'), may hold values from -1.8 to 1.8
Outputs:
- restored: float32 [1024, 2048], P('row', 'col')
- blur_dual_out: float32 [1024, 2048], P('row', 'col')
Inputs may be any that keep to these rules, and one draw needn't show every extreme that they name: `psf_index`: each entry names a row of psf_table.
All inputs are finite; a program needn't handle non-finite values.
Results may differ from a plain program's by a relative error of at most 0.0003.
Values may be sent and summed in bfloat16 or wider, within the bound.
A program may use at most 128 MiB of HBM per device.

v0:
```python
import jax
import jax.numpy as jnp
from jax import lax
from jax.sharding import PartitionSpec as P

ITERS = 2


sigma_step = 0.15
tau_step = 0.6
tv_weight = 0.5
group_size = 4


def for_sending(value):

    def short(part):
        return part.astype(jnp.bfloat16) if part.dtype == jnp.float32 else part

    return jax.tree.map(short, value)


def from_behind(block, axis, distance):
    devices = range(lax.axis_size(axis))
    route = [(i - distance, i) for i in devices if i - distance in devices]
    return lax.ppermute(block, axis, route)


def extended_2(cells, sides, width):
    for axis, dim in sides:
        count = lax.axis_size(axis)
        ends = count - 1
        head = lax.slice_in_dim(cells, 0, width, axis=dim)
        tail = lax.slice_in_dim(cells, cells.shape[dim] - width, cells.shape[dim], axis=dim)
        cells = jnp.concatenate(
            [
                lax.ppermute(tail, axis, [(i, (i + 1) % count) for i in range(ends)]),
                cells,
                lax.ppermute(head, axis, [((i + 1) % count, i) for i in range(ends)]),
            ],
            axis=dim,
        )
    return cells


def make_select(kernel_size, patch_cols):
    half_width = kernel_size // 2
    column_in = jnp.arange(patch_cols + 2 * half_width, dtype=jnp.int32)[None, :, None]
    column_out = jnp.arange(patch_cols, dtype=jnp.int32)[None, None, :]
    tap_index = jnp.arange(kernel_size, dtype=jnp.int32)[:, None, None]
    return (column_in - column_out == tap_index).astype(jnp.bfloat16)


def strip_pass(strip_in, observed_s, dual_s, index_s, kern_flat, select):
    kernel_size = select.shape[0]
    patch_cols = select.shape[2]
    half_width = (select.shape[1] - patch_cols) // 2
    patch_rows, width = observed_s.shape
    group_span = group_size * patch_cols
    group_count = width // group_span
    table_size = kern_flat.shape[0]

    def one_group(spread_sum, group_id):
        pieces = jnp.stack(
            [
                strip_in[:, member * patch_cols : member * patch_cols + patch_cols + 2 * half_width]
                for member in range(group_size)
            ]
        )
        stacked = jnp.stack(
            [pieces[:, tap_row : tap_row + patch_rows, :] for tap_row in range(kernel_size)], axis=2
        )
        onehot = (index_s[:, None] == jnp.arange(table_size, dtype=jnp.int32)[None, :]).astype(
            jnp.bfloat16
        )
        kernels = jnp.dot(onehot, kern_flat, preferred_element_type=jnp.float32).astype(
            jnp.bfloat16
        )
        kernels = kernels.reshape(group_size, kernel_size, kernel_size)
        toeplitz = jnp.einsum(
            "pab,bkj->pakj", kernels, select, preferred_element_type=jnp.float32
        ).astype(jnp.bfloat16)
        blurred = jnp.einsum(
            "piak,pakj->pij", stacked, toeplitz, preferred_element_type=jnp.float32
        )
        blurred = blurred.transpose(1, 0, 2).reshape(patch_rows, group_span)
        dual_new = (dual_s + sigma_step * (blurred - observed_s)) / (1.0 + sigma_step)
        rounded = (
            dual_new.astype(jnp.bfloat16)
            .reshape(patch_rows, group_size, patch_cols)
            .transpose(1, 0, 2)
        )
        padded_dual = jnp.pad(rounded, ((0, 0), (kernel_size - 1, kernel_size - 1), (0, 0)))
        shifted = jnp.stack(
            [
                padded_dual[
                    :,
                    kernel_size
                    - 1
                    - tap_row : kernel_size
                    - 1
                    - tap_row
                    + patch_rows
                    + 2 * half_width,
                    :,
                ]
                for tap_row in range(kernel_size)
            ],
            axis=2,
        )
        spread = jnp.einsum("praj,pakj->prk", shifted, toeplitz, preferred_element_type=jnp.float32)
        merged = jnp.zeros((patch_rows + 2 * half_width, group_span + 2 * half_width), jnp.float32)
        for member in range(group_size):
            merged = merged.at[
                :, member * patch_cols : member * patch_cols + patch_cols + 2 * half_width
            ].add(spread[member])
        previous = spread_sum
        spread_sum = previous + merged
        return (spread_sum, dual_new)

    start_sum = jnp.zeros((patch_rows + 2 * half_width, width + 2 * half_width), jnp.float32)
    spread_sum, duals = lax.scan(one_group, start_sum, jnp.arange(group_count, dtype=jnp.int32))
    return (duals.transpose(1, 0, 2).reshape(patch_rows, width), spread_sum)


def fold_rows(extended, extra, half_width):
    above_rim, above_extra = (
        from_behind(extended[-half_width:].astype(jnp.bfloat16), "row", 1).astype(jnp.float32),
        from_behind(for_sending(extra), "row", 1).astype(extra.dtype),
    )
    below_rim = from_behind(extended[:half_width], "row", -1)
    middle = extended[half_width:-half_width]
    middle = middle.at[:half_width].add(above_rim)
    middle = middle.at[-half_width:].add(below_rim)
    return (middle, above_extra)


def fold_cols(extended, extra, half_width):
    left_rim, left_extra = from_behind((extended[:, -half_width:], extra), "col", 1)
    right_rim = from_behind(extended[:, :half_width], "col", -1)
    middle = extended[:, half_width:-half_width]
    middle = middle.at[:, :half_width].add(left_rim)
    middle = middle.at[:, -half_width:].add(right_rim)
    return (middle, left_extra)


def per_device(observed, psf_table, psf_index, start_image, blur_dual, tv_dual):
    kernel_size = psf_table.shape[1]
    half_width = kernel_size // 2
    tile_rows, tile_cols = observed.shape
    table_size = psf_table.shape[0]
    table = psf_table.astype(jnp.float32)
    normed = table / jnp.sum(table, axis=(1, 2), keepdims=True)
    kern_flat = normed.astype(jnp.bfloat16).reshape(table_size, kernel_size * kernel_size)
    patch_cols = tile_cols // psf_index.shape[1]
    select = make_select(kernel_size, patch_cols)
    row_place = lax.axis_index("row") * tile_rows + jnp.arange(tile_rows, dtype=jnp.int32)
    col_place = lax.axis_index("col") * tile_cols + jnp.arange(tile_cols, dtype=jnp.int32)
    keep_rows = (row_place < tile_rows * lax.axis_size("row") - 1)[:, None]
    keep_cols = (col_place < tile_cols * lax.axis_size("col") - 1)[None, :]
    restored = start_image
    extrapolated = start_image
    dual_now = blur_dual
    tv_rows = tv_dual[0]
    tv_cols = tv_dual[1]
    for step in range(ITERS):
        padded = extended_2(extrapolated, (("row", 0), ("col", 1)), half_width)
        strip_in = padded.astype(jnp.bfloat16)
        below = padded[
            half_width + 1 : half_width + 1 + tile_rows, half_width : half_width + tile_cols
        ]
        right = padded[
            half_width : half_width + tile_rows, half_width + 1 : half_width + 1 + tile_cols
        ]
        grad_rows = jnp.where(keep_rows, below - extrapolated, 0.0)
        grad_cols = jnp.where(keep_cols, right - extrapolated, 0.0)
        dual_now, spread_sum = strip_pass(
            strip_in, observed, dual_now, psf_index[0], kern_flat, select
        )
        moved_rows = tv_rows + sigma_step * grad_rows
        moved_cols = tv_cols + sigma_step * grad_cols
        shrink = jnp.maximum(
            1.0, jnp.sqrt(moved_rows * moved_rows + moved_cols * moved_cols) / tv_weight
        )
        tv_rows = moved_rows / shrink
        tv_cols = moved_cols / shrink
        masked_rows = jnp.where(keep_rows, tv_rows, 0.0)
        masked_cols = jnp.where(keep_cols, tv_cols, 0.0)
        middle, edge_col = fold_cols(spread_sum, masked_cols[:, -1:], half_width)
        adjoint, edge_row = fold_rows(middle, masked_rows[-1:], half_width)
        diverge = masked_rows - jnp.concatenate([edge_row, masked_rows[:-1]], axis=0)
        diverge = diverge + masked_cols - jnp.concatenate([edge_col, masked_cols[:, :-1]], axis=1)
        next_image = restored - tau_step * (adjoint - diverge)
        extrapolated = 2.0 * next_image - restored
        restored = next_image
    return (restored, dual_now)


def solution(mesh):
    placed = (
        P("row", "col"),
        P(),
        P("row", "col"),
        P("row", "col"),
        P("row", "col"),
        P(None, "row", "col"),
    )
    return jax.shard_map(
        per_device,
        mesh=mesh,
        in_specs=placed,
        out_specs=(P("row", "col"), P("row", "col")),
        check_vma=False,
    )
```

profile of v0, /device:TPU:11, one launch (start us, length us, event | category | flops | bytes accessed | tf_op | source)
XLA Modules:
  0.0 152.2 jit_solution(3014836098553810146)
XLA Ops:
  1.6 3.7 %collective-permute-start = (f32[15,512]{0,1:T(8,128)S(1)}, f32[15,512]{0,1:T(8,128)S(1)}, u32[]{:S(2)}, u32[]{:S(2)}) collective-permute-start(f32[15,512]{0,1:T(8,128)S(1)} %copy.248), channel_id=1, source_target_pairs={{0,4},{4,8},{8,12},{12,16},{16,20},{20,24},{24,28},{1,5},{5,9},{9,... | collective-permute-start | bytes 92168 | tf_op jit(solution)/shard_map/ppermute | solution.py:37
  10.6 3.8 %convolution_convert_fusion = bf16[4,31,158,128]{3,1,2,0:T(8,128)(2,1)} fusion(s32[158,128]{1,0:T(8,128)S(1)} %iota_subtract_fusion, bf16[4,31,31,1]{2,1,0,3:T(8,128)(2,1)S(1)} %reshape.545), kind=kOutput, calls=%fused_computation.8 | convolution fusion | flops 158616832 | bytes 5104136 | tf_op jit(solution)/shard_map/while/body/eval_jaxpr/pab,bkj->pakj/dot_general | solution.py:80
  15.0 2.1 %collective-permute-start.3 = (f32[158,15]{0,1:T(8,128)S(1)}, f32[158,15]{0,1:T(8,128)S(1)}, u32[]{:S(2)}, u32[]{:S(2)}) collective-permute-start(f32[158,15]{0,1:T(8,128)S(1)} %slice.1229), channel_id=1, source_target_pairs={{1,0},{2,1},{3,2},{5,4},{6,5},{7,6},{9,8},{10,9},{11,10},{13,12},{... | collective-permute-start | bytes 28448 | tf_op jit(solution)/shard_map/ppermute | solution.py:39
  17.1 3.2 %collective-permute-start.2 = (bf16[158,15]{0,1:T(8,128)(2,1)S(1)}, bf16[158,15]{0,1:T(8,128)(2,1)S(1)}, u32[]{:S(2)}, u32[]{:S(2)}) collective-permute-start(bf16[158,15]{0,1:T(8,128)(2,1)S(1)} %slice.1226), channel_id=1, source_target_pairs={{0,1},{1,2},{2,3},{4,5},{5,6},{6,7},{8,9},{9,10},{10,11},{12,13},{... | collective-permute-start | bytes 14228 | tf_op jit(solution)/shard_map/ppermute | solution.py:37
  20.3 8.8 %copy.382 = bf16[4,31,158,128]{3,0,2,1:T(4,128)(2,1)} copy(bf16[4,31,158,128]{3,1,2,0:T(8,128)(2,1)} %convolution_convert_fusion) | data formatting | bytes 10031104
  36.3 1.9 %fusion.6 = f32[4,128,128,1]{1,2,3,0:T(8,128)S(1)} fusion(bf16[4,128,31,158]{1,3,2,0:T(8,128)(2,1)S(1)} %constant_dynamic-update-slice_fusion, bf16[4,31,158,128]{3,0,2,1:T(4,128)(2,1)S(1)} %copy-done), kind=kOutput, calls=%fused_computation.6 | convolution fusion | flops 641990656 | bytes 10293248 | tf_op jit(solution)/shard_map/while/body/eval_jaxpr/piak,pakj->pij/dot_general | solution.py:83
  40.1 4.0 %fusion.11 = f32[4,158,158]{1,2,0:T(8,128)S(1)} fusion(bf16[4,158,31,128]{3,1,2,0:T(8,128)(2,1)S(1)} %constant_dynamic-update-slice_fusion.31, bf16[4,31,158,128]{3,0,2,1:T(4,128)(2,1)} %copy.382), kind=kOutput, calls=%fused_computation.12 | convolution fusion | flops 792457216 | bytes 10430528 | tf_op jit(solution)/shard_map/while/body/eval_jaxpr/praj,pakj->prk/dot_general | solution.py:111
  48.6 3.2 %collective-permute-start.4 = (f32[158,15]{0,1:T(8,128)S(1)}, f32[158,15]{0,1:T(8,128)S(1)}, u32[]{:S(2)}, u32[]{:S(2)}) collective-permute-start(f32[158,15]{0,1:T(8,128)S(1)} %slice.1269), channel_id=1, source_target_pairs={{0,1},{1,2},{2,3},{4,5},{5,6},{6,7},{8,9},{9,10},{10,11},{12,13},{... | collective-permute-start | bytes 28448 | tf_op jit(solution)/shard_map/ppermute | solution.py:26
  56.1 2.0 %collective-permute-done.5 = f32[158,15]{0,1:T(8,128)S(1)} collective-permute-done((f32[158,15]{0,1:T(8,128)S(1)}, f32[158,15]{0,1:T(8,128)S(1)}, u32[]{:S(2)}, u32[]{:S(2)}) %collective-permute-start.5) | collective-permute-done | bytes 9512 | tf_op jit(solution)/shard_map/ppermute | solution.py:26
  58.4 7.4 %collective-permute-start.6 = (bf16[15,512]{0,1:T(8,128)(2,1)S(1)}, bf16[15,512]{0,1:T(8,128)(2,1)S(1)}, u32[]{:S(2)}, u32[]{:S(2)}) collective-permute-start(bf16[15,512]{0,1:T(8,128)(2,1)S(1)} %slice.1883), channel_id=1, source_target_pairs={{0,4},{4,8},{8,12},{12,16},{16,20},{20,24},{24,28},{1,5},{5,9},{9,... | collective-permute-start | bytes 46088 | tf_op jit(solution)/shard_map/ppermute | solution.py:26
  70.0 2.4 %collective-permute-start.7 = (f32[15,512]{0,1:T(8,128)}, f32[15,512]{0,1:T(8,128)S(1)}, u32[]{:S(2)}, u32[]{:S(2)}) collective-permute-start(f32[15,512]{0,1:T(8,128)} %get-tuple-element.315), channel_id=1, source_target_pairs={{4,0},{8,4},{12,8},{16,12},{20,16},{24,20},{28,24},{5,1},{9,5},{13... | collective-permute-start | bytes 92168 | tf_op jit(solution)/shard_map/ppermute | solution.py:26
  72.5 3.2 %collective-permute-start.9 = (f32[128,1]{0,1:T(1,128)S(1)}, f32[128,1]{0,1:T(1,128)S(1)}, u32[]{:S(2)}, u32[]{:S(2)}) collective-permute-start(f32[128,1]{0,1:T(1,128)S(1)} %slice.1279), channel_id=1, source_target_pairs={{0,1},{1,2},{2,3},{4,5},{5,6},{6,7},{8,9},{9,10},{10,11},{12,13},{... | collective-permute-start | bytes 1544 | tf_op jit(solution)/shard_map/ppermute | solution.py:26
  80.7 2.8 %collective-permute-start.10 = (f32[15,512]{0,1:T(8,128)S(1)}, f32[15,512]{0,1:T(8,128)S(1)}, u32[]{:S(2)}, u32[]{:S(2)}) collective-permute-start(f32[15,512]{0,1:T(8,128)S(1)} %get-tuple-element.321), channel_id=1, source_target_pairs={{0,4},{4,8},{8,12},{12,16},{16,20},{20,24},{24,28},{1,5},{5,9},{9,... | collective-permute-start | bytes 92168 | tf_op jit(solution)/shard_map/ppermute | solution.py:37
  85.5 2.2 %collective-permute-done.10 = f32[15,512]{0,1:T(8,128)S(1)} collective-permute-done((f32[15,512]{0,1:T(8,128)S(1)}, f32[15,512]{0,1:T(8,128)S(1)}, u32[]{:S(2)}, u32[]{:S(2)}) %collective-permute-start.10) | collective-permute-done | bytes 30752 | tf_op jit(solution)/shard_map/ppermute | solution.py:37
  87.7 4.4 %collective-permute-done.11 = f32[15,512]{0,1:T(8,128)S(1)} collective-permute-done((f32[15,512]{0,1:T(8,128)S(1)}, f32[15,512]{0,1:T(8,128)S(1)}, u32[]{:S(2)}, u32[]{:S(2)}) %collective-permute-start.11) | collective-permute-done | bytes 30752 | tf_op jit(solution)/shard_map/ppermute | solution.py:39
  92.4 2.1 %collective-permute-start.13 = (f32[158,15]{0,1:T(8,128)S(1)}, f32[158,15]{0,1:T(8,128)S(1)}, u32[]{:S(2)}, u32[]{:S(2)}) collective-permute-start(f32[158,15]{0,1:T(8,128)S(1)} %slice.1286), channel_id=1, source_target_pairs={{1,0},{2,1},{3,2},{5,4},{6,5},{7,6},{9,8},{10,9},{11,10},{13,12},{... | collective-permute-start | bytes 28448 | tf_op jit(solution)/shard_map/ppermute | solution.py:39
  94.5 3.4 %collective-permute-start.12 = (bf16[158,15]{0,1:T(8,128)(2,1)S(1)}, bf16[158,15]{0,1:T(8,128)(2,1)S(1)}, u32[]{:S(2)}, u32[]{:S(2)}) collective-permute-start(bf16[158,15]{0,1:T(8,128)(2,1)S(1)} %slice.1283), channel_id=1, source_target_pairs={{0,1},{1,2},{2,3},{4,5},{5,6},{6,7},{8,9},{9,10},{10,11},{12,13},{... | collective-permute-start | bytes 14228 | tf_op jit(solution)/shard_map/ppermute | solution.py:37
  108.1 4.0 %fusion.14 = f32[4,158,158]{1,2,0:T(8,128)S(1)} fusion(bf16[4,158,31,128]{3,1,2,0:T(8,128)(2,1)S(1)} %constant_dynamic-update-slice_fusion.93, bf16[4,31,158,128]{3,0,2,1:T(4,128)(2,1)} %copy.382), kind=kOutput, calls=%fused_computation.13 | convolution fusion | flops 792457216 | bytes 10430528 | tf_op jit(solution)/shard_map/while/body/eval_jaxpr/praj,pakj->prk/dot_general | solution.py:111
  118.5 3.2 %collective-permute-start.14 = (f32[158,15]{0,1:T(8,128)S(1)}, f32[158,15]{0,1:T(8,128)S(1)}, u32[]{:S(2)}, u32[]{:S(2)}) collective-permute-start(f32[158,15]{0,1:T(8,128)S(1)} %slice.1326), channel_id=1, source_target_pairs={{0,1},{1,2},{2,3},{4,5},{5,6},{6,7},{8,9},{9,10},{10,11},{12,13},{... | collective-permute-start | bytes 28448 | tf_op jit(solution)/shard_map/ppermute | solution.py:26
  125.9 2.3 %collective-permute-done.15 = f32[158,15]{0,1:T(8,128)S(1)} collective-permute-done((f32[158,15]{0,1:T(8,128)S(1)}, f32[158,15]{0,1:T(8,128)S(1)}, u32[]{:S(2)}, u32[]{:S(2)}) %collective-permute-start.15) | collective-permute-done | bytes 9512 | tf_op jit(solution)/shard_map/ppermute | solution.py:26
  128.4 5.4 %collective-permute-start.16 = (bf16[15,512]{0,1:T(8,128)(2,1)S(1)}, bf16[15,512]{0,1:T(8,128)(2,1)S(1)}, u32[]{:S(2)}, u32[]{:S(2)}) collective-permute-start(bf16[15,512]{0,1:T(8,128)(2,1)S(1)} %slice.1881), channel_id=1, source_target_pairs={{0,4},{4,8},{8,12},{12,16},{16,20},{20,24},{24,28},{1,5},{5,9},{9,... | collective-permute-start | bytes 46088 | tf_op jit(solution)/shard_map/ppermute | solution.py:26
  136.5 2.4 %collective-permute-start.17 = (f32[15,512]{0,1:T(8,128)}, f32[15,512]{0,1:T(8,128)S(1)}, u32[]{:S(2)}, u32[]{:S(2)}) collective-permute-start(f32[15,512]{0,1:T(8,128)} %get-tuple-element.311), channel_id=1, source_target_pairs={{4,0},{8,4},{12,8},{16,12},{20,16},{24,20},{28,24},{5,1},{9,5},{13... | collective-permute-start | bytes 92168 | tf_op jit(solution)/shard_map/ppermute | solution.py:26
  139.5 4.8 %collective-permute-start.18 = (bf16[1,512]{0,1:T(8,128)(2,1)S(1)}, bf16[1,512]{0,1:T(8,128)(2,1)S(1)}, u32[]{:S(2)}, u32[]{:S(2)}) collective-permute-start(bf16[1,512]{0,1:T(8,128)(2,1)S(1)} %slice.1880), channel_id=1, source_target_pairs={{0,4},{4,8},{8,12},{12,16},{16,20},{20,24},{24,28},{1,5},{5,9},{9,... | collective-permute-start | bytes 3080 | tf_op jit(solution)/shard_map/ppermute | solution.py:26
  144.2 3.2 %collective-permute-start.19 = (f32[128,1]{0,1:T(1,128)S(1)}, f32[128,1]{0,1:T(1,128)S(1)}, u32[]{:S(2)}, u32[]{:S(2)}) collective-permute-start(f32[128,1]{0,1:T(1,128)S(1)} %slice.1336), channel_id=1, source_target_pairs={{0,1},{1,2},{2,3},{4,5},{5,6},{6,7},{8,9},{9,10},{10,11},{12,13},{... | collective-permute-start | bytes 1544 | tf_op jit(solution)/shard_map/ppermute | solution.py:26
  (261 shorter events, 64.2 us)
Async XLA Ops:
  0.6 13.9 %copy-start.7 = (f32[128,512]{1,0:T(8,128)S(1)}, f32[128,512]{1,0:T(8,128)}, u32[]{:S(2)}) copy-start(f32[128,512]{1,0:T(8,128)} %param.41) | copy-start | bytes 786436
  0.6 13.8 %copy-start.6 = (f32[2,128,512]{2,1,0:T(8,128)S(1)}, f32[2,128,512]{2,1,0:T(8,128)}, u32[]{:S(2)}) copy-start(f32[2,128,512]{2,1,0:T(8,128)} %param.43) | copy-start | bytes 1572868
  1.6 13.0 %collective-permute-start = (f32[15,512]{0,1:T(8,128)S(1)}, f32[15,512]{0,1:T(8,128)S(1)}, u32[]{:S(2)}, u32[]{:S(2)}) collective-permute-start(f32[15,512]{0,1:T(8,128)S(1)} %copy.248), channel_id=1, source_target_pairs={{0,4},{4,8},{8,12},{12,16},{16,20},{20,24},{24,28},{1,5},{5,9},{9,... | collective-permute-start | bytes 92168 | tf_op jit(solution)/shard_map/ppermute | solution.py:37
  5.5 9.2 %collective-permute-start.1 = (f32[15,512]{0,1:T(8,128)S(1)}, f32[15,512]{0,1:T(8,128)S(1)}, u32[]{:S(2)}, u32[]{:S(2)}) collective-permute-start(f32[15,512]{0,1:T(8,128)S(1)} %copy.249), channel_id=1, source_target_pairs={{4,0},{8,4},{12,8},{16,12},{20,16},{24,20},{28,24},{5,1},{9,5},{13... | collective-permute-start | bytes 92168 | tf_op jit(solution)/shard_map/ppermute | solution.py:39
  15.0 16.6 %collective-permute-start.3 = (f32[158,15]{0,1:T(8,128)S(1)}, f32[158,15]{0,1:T(8,128)S(1)}, u32[]{:S(2)}, u32[]{:S(2)}) collective-permute-start(f32[158,15]{0,1:T(8,128)S(1)} %slice.1229), channel_id=1, source_target_pairs={{1,0},{2,1},{3,2},{5,4},{6,5},{7,6},{9,8},{10,9},{11,10},{13,12},{... | collective-permute-start | bytes 28448 | tf_op jit(solution)/shard_map/ppermute | solution.py:39
  17.1 14.6 %collective-permute-start.2 = (bf16[158,15]{0,1:T(8,128)(2,1)S(1)}, bf16[158,15]{0,1:T(8,128)(2,1)S(1)}, u32[]{:S(2)}, u32[]{:S(2)}) collective-permute-start(bf16[158,15]{0,1:T(8,128)(2,1)S(1)} %slice.1226), channel_id=1, source_target_pairs={{0,1},{1,2},{2,3},{4,5},{5,6},{6,7},{8,9},{9,10},{10,11},{12,13},{... | collective-permute-start | bytes 14228 | tf_op jit(solution)/shard_map/ppermute | solution.py:37
  48.6 4.5 %collective-permute-start.4 = (f32[158,15]{0,1:T(8,128)S(1)}, f32[158,15]{0,1:T(8,128)S(1)}, u32[]{:S(2)}, u32[]{:S(2)}) collective-permute-start(f32[158,15]{0,1:T(8,128)S(1)} %slice.1269), channel_id=1, source_target_pairs={{0,1},{1,2},{2,3},{4,5},{5,6},{6,7},{8,9},{9,10},{10,11},{12,13},{... | collective-permute-start | bytes 28448 | tf_op jit(solution)/shard_map/ppermute | solution.py:26
  53.6 4.5 %collective-permute-start.5 = (f32[158,15]{0,1:T(8,128)S(1)}, f32[158,15]{0,1:T(8,128)S(1)}, u32[]{:S(2)}, u32[]{:S(2)}) collective-permute-start(f32[158,15]{0,1:T(8,128)S(1)} %get-tuple-element.309), channel_id=1, source_target_pairs={{1,0},{2,1},{3,2},{5,4},{6,5},{7,6},{9,8},{10,9},{11,10},{13,12},{... | collective-permute-start | bytes 28448 | tf_op jit(solution)/shard_map/ppermute | solution.py:26
  58.4 10.8 %collective-permute-start.6 = (bf16[15,512]{0,1:T(8,128)(2,1)S(1)}, bf16[15,512]{0,1:T(8,128)(2,1)S(1)}, u32[]{:S(2)}, u32[]{:S(2)}) collective-permute-start(bf16[15,512]{0,1:T(8,128)(2,1)S(1)} %slice.1883), channel_id=1, source_target_pairs={{0,4},{4,8},{8,12},{12,16},{16,20},{20,24},{24,28},{1,5},{5,9},{9,... | collective-permute-start | bytes 46088 | tf_op jit(solution)/shard_map/ppermute | solution.py:26
  67.3 8.5 %collective-permute-start.8 = (bf16[1,512]{0,1:T(8,128)(2,1)S(1)}, bf16[1,512]{0,1:T(8,128)(2,1)S(1)}, u32[]{:S(2)}, u32[]{:S(2)}) collective-permute-start(bf16[1,512]{0,1:T(8,128)(2,1)S(1)} %slice.1882), channel_id=1, source_target_pairs={{0,4},{4,8},{8,12},{12,16},{16,20},{20,24},{24,28},{1,5},{5,9},{9,... | collective-permute-start | bytes 3080 | tf_op jit(solution)/shard_map/ppermute | solution.py:26
  70.0 8.8 %collective-permute-start.7 = (f32[15,512]{0,1:T(8,128)}, f32[15,512]{0,1:T(8,128)S(1)}, u32[]{:S(2)}, u32[]{:S(2)}) collective-permute-start(f32[15,512]{0,1:T(8,128)} %get-tuple-element.315), channel_id=1, source_target_pairs={{4,0},{8,4},{12,8},{16,12},{20,16},{24,20},{28,24},{5,1},{9,5},{13... | collective-permute-start | bytes 92168 | tf_op jit(solution)/shard_map/ppermute | solution.py:26
  72.5 7.8 %collective-permute-start.9 = (f32[128,1]{0,1:T(1,128)S(1)}, f32[128,1]{0,1:T(1,128)S(1)}, u32[]{:S(2)}, u32[]{:S(2)}) collective-permute-start(f32[128,1]{0,1:T(1,128)S(1)} %slice.1279), channel_id=1, source_target_pairs={{0,1},{1,2},{2,3},{4,5},{5,6},{6,7},{8,9},{9,10},{10,11},{12,13},{... | collective-permute-start | bytes 1544 | tf_op jit(solution)/shard_map/ppermute | solution.py:26
  80.4 23.2 %slice-start = ((s8[5015552]{0:T(1024)(128)(4,1)}), s8[4194304]{0:T(1024)(128)(4,1)S(1)}, s32[]{:S(2)}) async-start(s8[5015552]{0:T(1024)(128)(4,1)} %bitcast.853), calls=%async_computation | async-start | bytes 8388608
  80.7 7.0 %collective-permute-start.10 = (f32[15,512]{0,1:T(8,128)S(1)}, f32[15,512]{0,1:T(8,128)S(1)}, u32[]{:S(2)}, u32[]{:S(2)}) collective-permute-start(f32[15,512]{0,1:T(8,128)S(1)} %get-tuple-element.321), channel_id=1, source_target_pairs={{0,4},{4,8},{8,12},{12,16},{16,20},{20,24},{24,28},{1,5},{5,9},{9,... | collective-permute-start | bytes 92168 | tf_op jit(solution)/shard_map/ppermute | solution.py:37
  83.5 8.6 %collective-permute-start.11 = (f32[15,512]{0,1:T(8,128)S(1)}, f32[15,512]{0,1:T(8,128)S(1)}, u32[]{:S(2)}, u32[]{:S(2)}) collective-permute-start(f32[15,512]{0,1:T(8,128)S(1)} %get-tuple-element.322), channel_id=1, source_target_pairs={{4,0},{8,4},{12,8},{16,12},{20,16},{24,20},{28,24},{5,1},{9,5},{13... | collective-permute-start | bytes 92168 | tf_op jit(solution)/shard_map/ppermute | solution.py:39
  92.4 5.5 %collective-permute-start.13 = (f32[158,15]{0,1:T(8,128)S(1)}, f32[158,15]{0,1:T(8,128)S(1)}, u32[]{:S(2)}, u32[]{:S(2)}) collective-permute-start(f32[158,15]{0,1:T(8,128)S(1)} %slice.1286), channel_id=1, source_target_pairs={{1,0},{2,1},{3,2},{5,4},{6,5},{7,6},{9,8},{10,9},{11,10},{13,12},{... | collective-permute-start | bytes 28448 | tf_op jit(solution)/shard_map/ppermute | solution.py:39
  94.5 4.4 %collective-permute-start.12 = (bf16[158,15]{0,1:T(8,128)(2,1)S(1)}, bf16[158,15]{0,1:T(8,128)(2,1)S(1)}, u32[]{:S(2)}, u32[]{:S(2)}) collective-permute-start(bf16[158,15]{0,1:T(8,128)(2,1)S(1)} %slice.1283), channel_id=1, source_target_pairs={{0,1},{1,2},{2,3},{4,5},{5,6},{6,7},{8,9},{9,10},{10,11},{12,13},{... | collective-permute-start | bytes 14228 | tf_op jit(solution)/shard_map/ppermute | solution.py:37
  112.1 35.4 %copy-start.3 = (f32[128,512]{0,1:T(8,128)S(1)}, f32[128,512]{0,1:T(8,128)}, u32[]{:S(2)}) copy-start(f32[128,512]{0,1:T(8,128)} %get-tuple-element.295) | copy-start | bytes 786436
  118.5 4.6 %collective-permute-start.14 = (f32[158,15]{0,1:T(8,128)S(1)}, f32[158,15]{0,1:T(8,128)S(1)}, u32[]{:S(2)}, u32[]{:S(2)}) collective-permute-start(f32[158,15]{0,1:T(8,128)S(1)} %slice.1326), channel_id=1, source_target_pairs={{0,1},{1,2},{2,3},{4,5},{5,6},{6,7},{8,9},{9,10},{10,11},{12,13},{... | collective-permute-start | bytes 28448 | tf_op jit(solution)/shard_map/ppermute | solution.py:26
  123.6 4.5 %collective-permute-start.15 = (f32[158,15]{0,1:T(8,128)S(1)}, f32[158,15]{0,1:T(8,128)S(1)}, u32[]{:S(2)}, u32[]{:S(2)}) collective-permute-start(f32[158,15]{0,1:T(8,128)S(1)} %get-tuple-element.307), channel_id=1, source_target_pairs={{1,0},{2,1},{3,2},{5,4},{6,5},{7,6},{9,8},{10,9},{11,10},{13,12},{... | collective-permute-start | bytes 28448 | tf_op jit(solution)/shard_map/ppermute | solution.py:26
  128.4 7.3 %collective-permute-start.16 = (bf16[15,512]{0,1:T(8,128)(2,1)S(1)}, bf16[15,512]{0,1:T(8,128)(2,1)S(1)}, u32[]{:S(2)}, u32[]{:S(2)}) collective-permute-start(bf16[15,512]{0,1:T(8,128)(2,1)S(1)} %slice.1881), channel_id=1, source_target_pairs={{0,4},{4,8},{8,12},{12,16},{16,20},{20,24},{24,28},{1,5},{5,9},{9,... | collective-permute-start | bytes 46088 | tf_op jit(solution)/shard_map/ppermute | solution.py:26
  136.5 13.1 %collective-permute-start.17 = (f32[15,512]{0,1:T(8,128)}, f32[15,512]{0,1:T(8,128)S(1)}, u32[]{:S(2)}, u32[]{:S(2)}) collective-permute-start(f32[15,512]{0,1:T(8,128)} %get-tuple-element.311), channel_id=1, source_target_pairs={{4,0},{8,4},{12,8},{16,12},{20,16},{24,20},{28,24},{5,1},{9,5},{13... | collective-permute-start | bytes 92168 | tf_op jit(solution)/shard_map/ppermute | solution.py:26
  139.5 8.8 %collective-permute-start.18 = (bf16[1,512]{0,1:T(8,128)(2,1)S(1)}, bf16[1,512]{0,1:T(8,128)(2,1)S(1)}, u32[]{:S(2)}, u32[]{:S(2)}) collective-permute-start(bf16[1,512]{0,1:T(8,128)(2,1)S(1)} %slice.1880), channel_id=1, source_target_pairs={{0,4},{4,8},{8,12},{12,16},{16,20},{20,24},{24,28},{1,5},{5,9},{9,... | collective-permute-start | bytes 3080 | tf_op jit(solution)/shard_map/ppermute | solution.py:26
  144.2 6.9 %collective-permute-start.19 = (f32[128,1]{0,1:T(1,128)S(1)}, f32[128,1]{0,1:T(1,128)S(1)}, u32[]{:S(2)}, u32[]{:S(2)}) collective-permute-start(f32[128,1]{0,1:T(1,128)S(1)} %slice.1336), channel_id=1, source_target_pairs={{0,1},{1,2},{2,3},{4,5},{5,6},{6,7},{8,9},{9,10},{10,11},{12,13},{... | collective-permute-start | bytes 1544 | tf_op jit(solution)/shard_map/ppermute | solution.py:26
  (8 other events, 36.9 us)
where the time goes:
time: 153 us; the launch traced here: 152 us
  starting transfers between devices  62.1 us (41%)
  local copies, waits for them, and re-layouts  36 us (24%)
  waiting for transfers between devices  18.2 us (12%)
  other arithmetic  17.3 us (11%)
  matrix products  16.4 us (11%)
  between operations  2.17 us (1%)
    ppermute x12, starting transfers between devices, from_behind(): return lax.ppermute(block, axis, route)  40.9 us
    unnamed x152, local copies, waits for them, and re-layouts  22.4 us
    ppermute x4, starting transfers between devices, extended_2(): lax.ppermute(tail, axis, [(i, (i + 1) % count) for i in range(ends)])  13.2 us
    ppermute x12, waiting for transfers between devices, from_behind(): return lax.ppermute(block, axis, route)  10.5 us
    ppermute x4, starting transfers between devices, extended_2(): lax.ppermute(head, axis, [((i + 1) % count, i) for i in range(ends)])  7.99 us
    dot_general x2, matrix products, one_group(): jnp.einsum('praj,pakj->prk', shifted, toeplitz, preferred_element_type=jn...  7.93 us
    another operation x13, other arithmetic  7.76 us
    scatter-add x8, local copies, waits for them, and re-layouts, one_group(): merged = merged.at[:, member * patch_cols:member * patch_cols + patch_col...  4.82 us
  transfers between devices with their start and end apart: 20, of which 9 were waited for; matrix products, arithmetic and copies ran while one was open for 19% of the time, Pallas kernels for 0%

commit v1 on v0

v1 whole, which is shorter than its diff:
```python
import functools

import jax
import jax.numpy as jnp
from jax import lax
from jax.experimental import pallas as pl
from jax.experimental.pallas import tpu as pltpu
from jax.sharding import PartitionSpec as P

ITERS = 2
SIGMA = 0.15
TAU = 0.6
TV_WEIGHT = 0.5
LANES = 128
GROUP = 16
MESH = pl.DeviceIdType.MESH

DIRECTIONS = ((-1, 0), (1, 0), (0, -1), (0, 1), (-1, -1), (-1, 1), (1, -1), (1, 1))
UP, DOWN, LEFT, RIGHT, UP_LEFT, UP_RIGHT, DOWN_LEFT, DOWN_RIGHT = range(8)
OPPOSITE = (DOWN, UP, RIGHT, LEFT, DOWN_RIGHT, DOWN_LEFT, UP_RIGHT, UP_LEFT)


def body(
    kernel_size,
    index_ref,
    observed_ref,
    table_ref,
    start_ref,
    dual_ref,
    tv_ref,
    restored_ref,
    dual_out_ref,
    taps,
    taps_back,
    weights,
    weights_rest,
    adjoint,
    adjoint_rest,
    stack,
    padded_dual,
    bars,
    sums,
    image,
    tv,
    got_rows,
    got_cols,
    got_corners,
    send_sem,
    recv_sem,
):
    half = kernel_size // 2
    rows, cols = observed_ref.shape
    patches = index_ref.shape[1]
    tiles = patches + 1
    wide = tiles * LANES
    tall = rows + 2 * GROUP
    reach = rows + GROUP
    last = wide - LANES
    row, col = lax.axis_index("row"), lax.axis_index("col")
    row_count, col_count = lax.axis_size("row"), lax.axis_size("col")

    def there(d):
        r, c = row + DIRECTIONS[d][0], col + DIRECTIONS[d][1]
        return (r >= 0) & (r < row_count) & (c >= 0) & (c < col_count)

    def device(d):
        return (row + DIRECTIONS[d][0], col + DIRECTIONS[d][1])

    got_rows[...] = jnp.zeros_like(got_rows)
    got_cols[...] = jnp.zeros_like(got_cols)
    got_corners[...] = jnp.zeros_like(got_corners)

    barrier = pltpu.get_barrier_semaphore()
    for d in range(8):

        @pl.when(there(d))
        def _():
            pl.semaphore_signal(barrier, inc=1, device_id=device(d), device_id_type=MESH)

    lane = lax.broadcasted_iota(jnp.int32, (1, LANES), 1)
    lane_wide = lax.broadcasted_iota(jnp.int32, (1, wide), 1)
    row_id = lax.broadcasted_iota(jnp.int32, (rows, 1), 0)
    own_lane = (lane_wide >= half) & (lane_wide < half + cols)
    keep_rows = (row_id < rows - 1) | (row < row_count - 1)
    keep_cols = (lane_wide < half + cols - 1) | (col < col_count - 1)

    def shifted(value):
        full = jnp.concatenate([value, jnp.zeros((rows, LANES), jnp.float32)], axis=1)
        return pltpu.roll(full, half, axis=1)

    start = shifted(start_ref[...])
    image[...] = start
    bars[0, :GROUP, :] = jnp.zeros((GROUP, wide), jnp.float32)
    bars[0, GROUP : GROUP + rows, :] = start
    bars[0, GROUP + rows :, :] = jnp.zeros((GROUP, wide), jnp.float32)

    tall_peers = (row > 0).astype(jnp.int32) + (row < row_count - 1).astype(jnp.int32)
    wide_peers = (col > 0).astype(jnp.int32) + (col < col_count - 1).astype(jnp.int32)
    pl.semaphore_wait(barrier, (tall_peers + 1) * (wide_peers + 1) - 1)

    inner = pl.ds(GROUP, rows)

    def copies(turn, source, low, high):
        row_part = {-1: low, 0: inner, 1: high}
        col_part = {-1: pl.ds(0, LANES), 0: pl.ds(0, wide), 1: pl.ds(last, LANES)}
        result = []
        for d, (dr, dc) in enumerate(DIRECTIONS):
            back = OPPOSITE[d]
            if d in (UP, DOWN):
                target = got_rows.at[turn, back - UP]
            elif d in (LEFT, RIGHT):
                target = got_cols.at[turn, back - LEFT]
            else:
                target = got_corners.at[turn, back - UP_LEFT]
            send = pltpu.make_async_remote_copy(
                src_ref=source.at[row_part[dr], col_part[dc]],
                dst_ref=target,
                send_sem=send_sem.at[turn, d],
                recv_sem=recv_sem.at[turn, back],
                device_id=device(d),
                device_id_type=MESH,
            )
            arrive = pltpu.make_async_remote_copy(
                src_ref=source.at[row_part[dr], col_part[dc]],
                dst_ref=(
                    got_rows.at[turn, d - UP]
                    if d in (UP, DOWN)
                    else got_cols.at[turn, d - LEFT]
                    if d in (LEFT, RIGHT)
                    else got_corners.at[turn, d - UP_LEFT]
                ),
                send_sem=send_sem.at[turn, d],
                recv_sem=recv_sem.at[turn, d],
                device_id=device(d),
                device_id_type=MESH,
            )
            result.append((send, arrive))
        return result

    def start_copies(made):
        for d in (LEFT, RIGHT, UP, DOWN, UP_LEFT, UP_RIGHT, DOWN_LEFT, DOWN_RIGHT):

            @pl.when(there(d))
            def _():
                made[d][0].start()

    def wait_copies(made):
        for d in range(8):

            @pl.when(there(d))
            def _():
                made[d][0].wait_send()
                made[d][1].wait_recv()

    image_low, image_high = pl.ds(GROUP, GROUP), pl.ds(rows, GROUP)
    sums_low, sums_high = pl.ds(0, GROUP), pl.ds(GROUP + rows, GROUP)

    exchange = copies(0, bars.at[0], image_low, image_high)
    start_copies(exchange)

    tv[0] = shifted(tv_ref[0])
    tv[1] = shifted(tv_ref[1])
    dual_out_ref[...] = dual_ref[...]
    padded_dual[...] = jnp.zeros_like(padded_dual)
    taps[...] = jnp.zeros_like(taps)
    turned = lax.broadcasted_iota(jnp.int32, (LANES, LANES), 0)
    column = lax.broadcasted_iota(jnp.int32, (LANES, LANES), 1)
    reverse = (((turned + column) == LANES) | ((turned + column) == 0)).astype(jnp.bfloat16)
    for patch in range(patches):
        entry = table_ref[index_ref[0, patch]].astype(jnp.float32)
        normed = (entry / jnp.sum(entry)).astype(jnp.bfloat16).astype(jnp.float32)
        taps[patch, :kernel_size, :kernel_size] = normed
        taps_back[patch] = jnp.dot(
            taps[patch].astype(jnp.bfloat16), reverse, preferred_element_type=jnp.float32
        )

    def circulant(base):
        return pltpu.roll(
            jnp.broadcast_to(base, (LANES, LANES)), 0, axis=1, stride=1, stride_axis=0
        )

    below_diagonal = column <= turned
    above_diagonal = column >= turned

    def build(step, carry):
        patch = step // GROUP
        shift = step % GROUP
        here = pl.ds(pl.multiple_of(shift * LANES, LANES), LANES)
        for n in range(2):
            span = pl.ds(n * LANES, LANES)
            base = taps_back[patch, pl.ds(n * GROUP + shift, 1), :]
            full = circulant(base)
            weights[patch, here, span] = jnp.where(below_diagonal, full, 0.0).astype(jnp.bfloat16)
            weights_rest[patch, here, span] = jnp.where(below_diagonal, 0.0, full).astype(
                jnp.bfloat16
            )
            base = taps[patch, pl.ds(n * GROUP + GROUP - 1 - shift, 1), :]
            full = circulant(base)
            adjoint[patch, here, span] = jnp.where(above_diagonal, full, 0.0).astype(jnp.bfloat16)
            adjoint_rest[patch, here, span] = jnp.where(above_diagonal, 0.0, full).astype(
                jnp.bfloat16
            )
        return carry

    lax.fori_loop(0, patches * GROUP, build, 0)

    wait_copies(exchange)

    for step in range(ITERS):
        turn = 2 * step
        bar = bars.at[step]
        total = sums.at[step]

        middle = pl.ds(GROUP, rows)
        tile_first, tile_last = pl.ds(0, LANES), pl.ds(last, LANES)
        in_left = lane < half
        bar[middle, tile_first] = jnp.where(in_left, got_cols[turn, 0], bar[middle, tile_first])
        bar[middle, tile_last] = jnp.where(in_left, bar[middle, tile_last], got_cols[turn, 1])
        for side, place in ((0, pl.ds(0, GROUP)), (1, pl.ds(GROUP + rows, GROUP))):
            bar[place, :] = got_rows[turn, side]
            bar[place, tile_first] = jnp.where(
                in_left, got_corners[turn, 2 * side], got_rows[turn, side, :, :LANES]
            )
            bar[place, tile_last] = jnp.where(
                in_left, got_rows[turn, side, :, last:], got_corners[turn, 2 * side + 1]
            )

        def stack_bar(tile, carry):
            here = pl.ds(pl.multiple_of(tile * LANES, LANES), LANES)
            for shift in range(GROUP):
                stack[tile, :, shift * LANES : (shift + 1) * LANES] = bar[
                    pl.ds(shift + 1, reach), here
                ].astype(jnp.bfloat16)
            return carry

        lax.fori_loop(0, tiles, stack_bar, 0)

        def blur(patch, carry):
            here = pl.ds(pl.multiple_of(patch * LANES, LANES), LANES)
            both = jnp.dot(stack[patch], weights[patch], preferred_element_type=jnp.float32)
            both += jnp.dot(
                stack[patch + 1], weights_rest[patch], preferred_element_type=jnp.float32
            )
            blurred = both[:rows, :LANES] + both[GROUP:, LANES:]
            dual = (dual_out_ref[:, here] + SIGMA * (blurred - observed_ref[:, here])) / (
                1.0 + SIGMA
            )
            dual_out_ref[:, here] = dual
            padded_dual[GROUP : GROUP + rows, here] = dual
            return carry

        lax.fori_loop(0, patches, blur, 0)

        def stack_dual(patch, carry):
            here = pl.ds(pl.multiple_of(patch * LANES, LANES), LANES)
            for shift in range(GROUP):
                stack[patch, :, shift * LANES : (shift + 1) * LANES] = padded_dual[
                    pl.ds(shift, reach), here
                ].astype(jnp.bfloat16)
            return carry

        lax.fori_loop(0, patches, stack_dual, 0)

        def put(tile, both):
            here = pl.ds(pl.multiple_of(tile * LANES, LANES), LANES)
            total[:GROUP, here] = both[:GROUP, :LANES]
            total[pl.ds(GROUP, rows), here] = both[GROUP:, :LANES] + both[:rows, LANES:]
            total[pl.ds(GROUP + rows, GROUP), here] = both[rows:, LANES:]

        put(0, jnp.dot(stack[0], adjoint[0], preferred_element_type=jnp.float32))

        def spread(tile, carry):
            both = jnp.dot(stack[tile], adjoint[tile], preferred_element_type=jnp.float32)
            both += jnp.dot(
                stack[tile - 1], adjoint_rest[tile - 1], preferred_element_type=jnp.float32
            )
            put(tile, both)
            return carry

        lax.fori_loop(1, patches, spread, 0)
        put(
            patches,
            jnp.dot(
                stack[patches - 1], adjoint_rest[patches - 1], preferred_element_type=jnp.float32
            ),
        )

        now = bar[middle, :]
        grad_rows = jnp.where(keep_rows, bar[pl.ds(GROUP + 1, rows), :] - now, 0.0)
        grad_cols = jnp.where(keep_cols, pltpu.roll(now, wide - 1, axis=1) - now, 0.0)
        moved_rows = tv[0] + SIGMA * grad_rows
        moved_cols = tv[1] + SIGMA * grad_cols
        shrink = jnp.maximum(
            1.0, jnp.sqrt(moved_rows * moved_rows + moved_cols * moved_cols) / TV_WEIGHT
        )
        new_rows = moved_rows / shrink
        new_cols = moved_cols / shrink
        tv[0] = new_rows
        tv[1] = new_cols
        masked_rows = jnp.where(keep_rows & own_lane, new_rows, 0.0)
        masked_cols = jnp.where(keep_cols & own_lane, new_cols, 0.0)
        total[middle, :] += pltpu.roll(masked_cols, 1, axis=1) - masked_cols - masked_rows
        total[pl.ds(GROUP + 1, rows), :] += masked_rows

        exchange = copies(turn + 1, total, sums_low, sums_high)
        start_copies(exchange)
        wait_copies(exchange)

        got = turn + 1
        total[middle, tile_first] += got_cols[got, 0]
        total[middle, tile_last] += got_cols[got, 1]
        for side, place in ((0, pl.ds(GROUP, GROUP)), (1, pl.ds(rows, GROUP))):
            total[place, :] += got_rows[got, side]
            total[place, tile_first] += got_corners[got, 2 * side]
            total[place, tile_last] += got_corners[got, 2 * side + 1]

        old = image[...]
        new = old - TAU * total[middle, :]
        if step < ITERS - 1:
            image[...] = new
            following = bars.at[step + 1]
            following[middle, :] = 2.0 * new - old
            exchange = copies(turn + 2, following, image_low, image_high)
            start_copies(exchange)
            wait_copies(exchange)
        else:
            restored_ref[...] = pltpu.roll(new, wide - half, axis=1)[:, :cols]


def per_device(observed, psf_table, psf_index, start_image, blur_dual, tv_dual):
    kernel_size = psf_table.shape[1]
    rows, cols = observed.shape
    patches = psf_index.shape[1]
    tiles = patches + 1
    wide = tiles * LANES
    turns = 2 * ITERS
    whole = pl.BlockSpec(memory_space=pltpu.VMEM)
    deep = GROUP * LANES
    weight = pltpu.VMEM((patches, deep, 2 * LANES), jnp.bfloat16)
    f32 = jnp.float32
    return pl.pallas_call(
        functools.partial(body, kernel_size),
        out_shape=(
            jax.ShapeDtypeStruct((rows, cols), f32),
            jax.ShapeDtypeStruct((rows, cols), f32),
        ),
        in_specs=[pl.BlockSpec(memory_space=pltpu.SMEM)] + [whole] * 5,
        out_specs=(whole, whole),
        scratch_shapes=[
            pltpu.VMEM((patches, 2 * GROUP, LANES), f32),
            pltpu.VMEM((patches, 2 * GROUP, LANES), f32),
            weight,
            weight,
            weight,
            weight,
            pltpu.VMEM((tiles, rows + GROUP, deep), jnp.bfloat16),
            pltpu.VMEM((rows + 2 * GROUP, cols), f32),
            pltpu.VMEM((ITERS, rows + 2 * GROUP, wide), f32),
            pltpu.VMEM((ITERS, rows + 2 * GROUP, wide), f32),
            pltpu.VMEM((rows, wide), f32),
            pltpu.VMEM((2, rows, wide), f32),
            pltpu.VMEM((turns, 2, GROUP, wide), f32),
            pltpu.VMEM((turns, 2, rows, LANES), f32),
            pltpu.VMEM((turns, 4, GROUP, LANES), f32),
            pltpu.SemaphoreType.DMA((turns, 8)),
            pltpu.SemaphoreType.DMA((turns, 8)),
        ],
        compiler_params=pltpu.CompilerParams(
            collective_id=0, has_side_effects=True, vmem_limit_bytes=60 * 1024 * 1024
        ),
    )(psf_index, observed, psf_table, start_image, blur_dual, tv_dual)


def solution(mesh):
    placed = (
        P("row", "col"),
        P(),
        P("row", "col"),
        P("row", "col"),
        P("row", "col"),
        P(None, "row", "col"),
    )
    return jax.shard_map(
        per_device,
        mesh=mesh,
        in_specs=placed,
        out_specs=(P("row", "col"), P("row", "col")),
        check_vma=False,
    )
```

time: 153 us -> 46 us (0.30)
  starting transfers between devices: 62.1 us -> 0 us
  Pallas kernels: 0 us -> 39.7 us
  local copies, waits for them, and re-layouts: 36 us -> 4.99 us
  waiting for transfers between devices: 18.2 us -> 0 us
  other arithmetic: 17.3 us -> 0 us
  matrix products: 16.4 us -> 0 us
    ppermute x20 -> x0, starting transfers between devices: 62.1 us -> none  [the longest x12 40.9 us: from_behind(): return lax.ppermute(block, axis, route)]
    pallas_call x0 -> x1, Pallas kernels: none -> 39.7 us  [per_device(): pl.pallas_call(functools.partial(body, kernel_size), out_shape=(jax.Shape...]
    ppermute x20 -> x0, waiting for transfers between devices: 18.2 us -> none  [the longest x12 10.5 us: from_behind(): return lax.ppermute(block, axis, route)]
    unnamed x152 -> x5, local copies, waits for them, and re-layouts: 22.4 us -> 4.99 us
    dot_general x6 -> x0, matrix products: 16.4 us -> none  [the longest x2 7.93 us: one_group(): jnp.einsum('praj,pakj->prk', shifted, toeplitz, preferred_element_type=jn...]
    scatter-add x16 -> x0, local copies, waits for them, and re-layouts: 10.6 us -> none  [the longest x8 4.82 us: one_group(): merged = merged.at[:, member * patch_cols:member * patch_cols + patch_col...]
    another operation x17 -> x0, other arithmetic: 8.09 us -> none
    slice x4 -> x0, other arithmetic: 2.65 us -> none  [the longest x2 1.51 us: fold_rows(): below_rim = from_behind(extended[:half_width], 'row', -1)]
  transfers between devices with their start and end apart: 20 -> 0, of which waited for: 9 -> 0; matrix products, arithmetic and copies ran while one was open for 19% -> 0% of each run, Pallas kernels for 0% -> 0%
where the time goes in v1:
time: 46 us; the launch traced here: 45.3 us
  Pallas kernels  39.7 us (86%)
  local copies, waits for them, and re-layouts  4.99 us (11%)
  between operations  0.65 us (1%)
    pallas_call x1, Pallas kernels, per_device(): pl.pallas_call(functools.partial(body, kernel_size), out_shape=(jax.Shape...  39.7 us
    unnamed x5, local copies, waits for them, and re-layouts  4.99 us

profile of v1, /device:TPU:11, one launch (start us, length us, event | category | flops | bytes accessed | tf_op | source)
XLA Modules:
  0.0 45.3 jit_solution(38063543640834021)
XLA Ops:
  0.6 2.6 %copy.8.table_ref = bf16[64,31,31]{2,1,0:T(8,128)(2,1)} copy(bf16[64,31,31]{0,2,1:T(8,128)(2,1)} %param.7) | data formatting | bytes 246016 | tf_op args[1]
  3.2 39.7 %shard_map.77 = (f32[128,512]{1,0:T(8,128)}, f32[128,512]{1,0:T(8,128)}) custom-call(s32[1,4]{1,0:T(1,128)} %index_ref.1, f32[128,512]{1,0:T(8,128)} %observed_ref.1, bf16[64,31,31]{2,1,0:T(8,128)(2,1)} %copy.8.table_ref, f32[128,512]{1,0:T(8,128)} %start_ref.1, f32[128,512]{1,0:T(8,128)} %dual_ref.1, f32[2,128,512]{2,1,0:T(8,128)} %tv_ref.1), custom_call_target="tpu_custom_call" | custom-call | tf_op jit(solution)/shard_map/pallas_call | solution.py:341
  42.9 0.0 copy-start
  42.9 1.7 %copy.11 = f32[128,512]{1,0:T(8,128)} copy(f32[128,512]{1,0:T(8,128)} %get-tuple-element.4) | data formatting | bytes 524288
  44.6 0.0 copy-done
  44.6 0.7 %copy.12 = f32[128,512]{1,0:T(8,128)} copy(f32[128,512]{1,0:T(8,128)S(1)} %copy-done) | data formatting | bytes 524288
Async XLA Ops:
  42.9 1.7 %copy-start = (f32[128,512]{1,0:T(8,128)S(1)}, f32[128,512]{1,0:T(8,128)}, u32[]{:S(2)}) copy-start(f32[128,512]{1,0:T(8,128)} %get-tuple-element.5) | copy-start | bytes 786436

commit v2 on v1

--- a/solution.py
+++ b/solution.py
@@ -23,10 +23,16 @@
 def body(
     kernel_size,
     index_ref,
+    observed_hbm,
+    table_hbm,
+    start_hbm,
+    dual_hbm,
+    tv_hbm,
+    restored_hbm,
+    dual_out_hbm,
     observed_ref,
     table_ref,
     start_ref,
-    dual_ref,
     tv_ref,
     restored_ref,
     dual_out_ref,
@@ -45,8 +51,10 @@
     got_rows,
     got_cols,
     got_corners,
+    sent_cols,
     send_sem,
     recv_sem,
+    load_sem,
 ):
     half = kernel_size // 2
     rows, cols = observed_ref.shape
@@ -66,6 +74,21 @@
     def device(d):
         return (row + DIRECTIONS[d][0], col + DIRECTIONS[d][1])
 
+    loads = [
+        pltpu.make_async_copy(source, target, load_sem.at[i])
+        for i, (source, target) in enumerate(
+            (
+                (start_hbm, start_ref),
+                (table_hbm, table_ref),
+                (tv_hbm, tv_ref),
+                (dual_hbm, dual_out_ref),
+                (observed_hbm, observed_ref),
+            )
+        )
+    ]
+    for load in loads:
+        load.start()
+
     got_rows[...] = jnp.zeros_like(got_rows)
     got_cols[...] = jnp.zeros_like(got_cols)
     got_corners[...] = jnp.zeros_like(got_corners)
@@ -88,6 +111,7 @@
         full = jnp.concatenate([value, jnp.zeros((rows, LANES), jnp.float32)], axis=1)
         return pltpu.roll(full, half, axis=1)
 
+    loads[0].wait()
     start = shifted(start_ref[...])
     image[...] = start
     bars[0, :GROUP, :] = jnp.zeros((GROUP, wide), jnp.float32)
@@ -112,8 +136,12 @@
                 target = got_cols.at[turn, back - LEFT]
             else:
                 target = got_corners.at[turn, back - UP_LEFT]
+            if d in (LEFT, RIGHT):
+                origin = sent_cols.at[turn, d - LEFT]
+            else:
+                origin = source.at[row_part[dr], col_part[dc]]
             send = pltpu.make_async_remote_copy(
-                src_ref=source.at[row_part[dr], col_part[dc]],
+                src_ref=origin,
                 dst_ref=target,
                 send_sem=send_sem.at[turn, d],
                 recv_sem=recv_sem.at[turn, back],
@@ -121,7 +149,7 @@
                 device_id_type=MESH,
             )
             arrive = pltpu.make_async_remote_copy(
-                src_ref=source.at[row_part[dr], col_part[dc]],
+                src_ref=origin,
                 dst_ref=(
                     got_rows.at[turn, d - UP]
                     if d in (UP, DOWN)
@@ -137,42 +165,77 @@
             result.append((send, arrive))
         return result
 
-    def start_copies(made):
-        for d in (LEFT, RIGHT, UP, DOWN, UP_LEFT, UP_RIGHT, DOWN_LEFT, DOWN_RIGHT):
+    def start_copies(made, which):
+        for d in which:
 
             @pl.when(there(d))
             def _():
                 made[d][0].start()
 
-    def wait_copies(made):
-        for d in range(8):
+    def wait_copies(made, which):
+        for d in which:
 
             @pl.when(there(d))
             def _():
                 made[d][0].wait_send()
                 made[d][1].wait_recv()
 
+    lane_group = lane // GROUP
+    groups = rows // GROUP
+
+    def pack(source, first, offset, target):
+        packed = jnp.zeros((GROUP, LANES), jnp.float32)
+        for g in range(groups):
+            part = source[GROUP + g * GROUP : 2 * GROUP + g * GROUP, first : first + LANES]
+            moved = pltpu.roll(part, (g * GROUP - offset) % LANES, axis=1)
+            packed = jnp.where(lane_group == g, moved, packed)
+        target[...] = packed
+
+    def unpack(packed, offset):
+        return jnp.concatenate(
+            [pltpu.roll(packed, (offset - g * GROUP) % LANES, axis=1) for g in range(groups)],
+            axis=0,
+        )
+
+    near, far = (UP, DOWN), (LEFT, RIGHT, UP_LEFT, UP_RIGHT, DOWN_LEFT, DOWN_RIGHT)
+
     image_low, image_high = pl.ds(GROUP, GROUP), pl.ds(rows, GROUP)
     sums_low, sums_high = pl.ds(0, GROUP), pl.ds(GROUP + rows, GROUP)
 
+    pack(bars.at[0], 0, half, sent_cols.at[0, 0])
+    pack(bars.at[0], last, 0, sent_cols.at[0, 1])
     exchange = copies(0, bars.at[0], image_low, image_high)
-    start_copies(exchange)
-
-    tv[0] = shifted(tv_ref[0])
-    tv[1] = shifted(tv_ref[1])
-    dual_out_ref[...] = dual_ref[...]
+    start_copies(exchange, far + near)
+
     padded_dual[...] = jnp.zeros_like(padded_dual)
-    taps[...] = jnp.zeros_like(taps)
     turned = lax.broadcasted_iota(jnp.int32, (LANES, LANES), 0)
     column = lax.broadcasted_iota(jnp.int32, (LANES, LANES), 1)
     reverse = (((turned + column) == LANES) | ((turned + column) == 0)).astype(jnp.bfloat16)
+    entries = table_ref.shape[2]
+    slot = lax.broadcasted_iota(jnp.int32, (8, entries), 0)
+    entry = lax.broadcasted_iota(jnp.int32, (8, entries), 1)
+    chosen = jnp.zeros((8, entries), jnp.float32)
     for patch in range(patches):
-        entry = table_ref[index_ref[0, patch]].astype(jnp.float32)
-        normed = (entry / jnp.sum(entry)).astype(jnp.bfloat16).astype(jnp.float32)
-        taps[patch, :kernel_size, :kernel_size] = normed
-        taps_back[patch] = jnp.dot(
-            taps[patch].astype(jnp.bfloat16), reverse, preferred_element_type=jnp.float32
-        )
+        hit = (slot == patch) & (entry == index_ref[0, patch])
+        chosen = jnp.where(hit, 1.0, chosen)
+    chosen = chosen.astype(jnp.bfloat16)
+    taps[...] = jnp.zeros_like(taps)
+    loads[1].wait()
+    for tap_row in range(kernel_size):
+        taps[tap_row, :, :kernel_size] = lax.dot_general(
+            chosen,
+            table_ref[tap_row],
+            (((1,), (1,)), ((), ())),
+            preferred_element_type=jnp.float32,
+        )
+    raw = taps[...]
+    weight_sum = jnp.sum(jnp.sum(raw, axis=0), axis=1, keepdims=True)
+    used = lax.broadcasted_iota(jnp.int32, (8, 1), 0) < patches
+    normed = (raw / jnp.where(used, weight_sum, 1.0)[None]).astype(jnp.bfloat16)
+    taps[...] = normed.astype(jnp.float32)
+    taps_back[...] = jnp.dot(
+        normed.reshape(2 * GROUP * 8, LANES), reverse, preferred_element_type=jnp.float32
+    ).reshape(2 * GROUP, 8, LANES)
 
     def circulant(base):
         return pltpu.roll(
@@ -188,13 +251,13 @@
         here = pl.ds(pl.multiple_of(shift * LANES, LANES), LANES)
         for n in range(2):
             span = pl.ds(n * LANES, LANES)
-            base = taps_back[patch, pl.ds(n * GROUP + shift, 1), :]
+            base = taps_back[n * GROUP + shift, pl.ds(patch, 1), :]
             full = circulant(base)
             weights[patch, here, span] = jnp.where(below_diagonal, full, 0.0).astype(jnp.bfloat16)
             weights_rest[patch, here, span] = jnp.where(below_diagonal, 0.0, full).astype(
                 jnp.bfloat16
             )
-            base = taps[patch, pl.ds(n * GROUP + GROUP - 1 - shift, 1), :]
+            base = taps[n * GROUP + GROUP - 1 - shift, pl.ds(patch, 1), :]
             full = circulant(base)
             adjoint[patch, here, span] = jnp.where(above_diagonal, full, 0.0).astype(jnp.bfloat16)
             adjoint_rest[patch, here, span] = jnp.where(above_diagonal, 0.0, full).astype(
@@ -204,26 +267,27 @@
 
     lax.fori_loop(0, patches * GROUP, build, 0)
 
-    wait_copies(exchange)
+    loads[2].wait()
+    tv[0] = shifted(tv_ref[0])
+    tv[1] = shifted(tv_ref[1])
+    loads[3].wait()
+    loads[4].wait()
+
+    middle = pl.ds(GROUP, rows)
+    tile_first, tile_last = pl.ds(0, LANES), pl.ds(last, LANES)
+    in_left = lane < half
+    top, bottom = pl.ds(0, GROUP), pl.ds(GROUP + rows, GROUP)
+    dual_store = pltpu.make_async_copy(dual_out_ref, dual_out_hbm, load_sem.at[0])
+    image_store = pltpu.make_async_copy(restored_ref, restored_hbm, load_sem.at[1])
 
     for step in range(ITERS):
         turn = 2 * step
         bar = bars.at[step]
         total = sums.at[step]
 
-        middle = pl.ds(GROUP, rows)
-        tile_first, tile_last = pl.ds(0, LANES), pl.ds(last, LANES)
-        in_left = lane < half
-        bar[middle, tile_first] = jnp.where(in_left, got_cols[turn, 0], bar[middle, tile_first])
-        bar[middle, tile_last] = jnp.where(in_left, bar[middle, tile_last], got_cols[turn, 1])
-        for side, place in ((0, pl.ds(0, GROUP)), (1, pl.ds(GROUP + rows, GROUP))):
-            bar[place, :] = got_rows[turn, side]
-            bar[place, tile_first] = jnp.where(
-                in_left, got_corners[turn, 2 * side], got_rows[turn, side, :, :LANES]
-            )
-            bar[place, tile_last] = jnp.where(
-                in_left, got_rows[turn, side, :, last:], got_corners[turn, 2 * side + 1]
-            )
+        wait_copies(exchange, near)
+        bar[top, :] = got_rows[turn, 0]
+        bar[bottom, :] = got_rows[turn, 1]
 
         def stack_bar(tile, carry):
             here = pl.ds(pl.multiple_of(tile * LANES, LANES), LANES)
@@ -233,7 +297,7 @@
                 ].astype(jnp.bfloat16)
             return carry
 
-        lax.fori_loop(0, tiles, stack_bar, 0)
+        lax.fori_loop(1, tiles - 1, stack_bar, 0)
 
         def blur(patch, carry):
             here = pl.ds(pl.multiple_of(patch * LANES, LANES), LANES)
@@ -249,7 +313,50 @@
             padded_dual[GROUP : GROUP + rows, here] = dual
             return carry
 
-        lax.fori_loop(0, patches, blur, 0)
+        lax.fori_loop(1, patches - 1, blur, 0)
+
+        wait_copies(exchange, far)
+        bar[middle, tile_first] = jnp.where(
+            in_left, unpack(got_cols[turn, 0], 0), bar[middle, tile_first]
+        )
+        in_right = (lane >= half) & (lane < half + GROUP)
+        bar[middle, tile_last] = jnp.where(
+            in_left,
+            bar[middle, tile_last],
+            jnp.where(in_right, unpack(got_cols[turn, 1], half), 0.0),
+        )
+        for side, place in ((0, top), (1, bottom)):
+            bar[place, tile_first] = jnp.where(
+                in_left, got_corners[turn, 2 * side], got_rows[turn, side, :, :LANES]
+            )
+            bar[place, tile_last] = jnp.where(
+                in_left, got_rows[turn, side, :, last:], got_corners[turn, 2 * side + 1]
+            )
+        stack_bar(0, 0)
+        stack_bar(tiles - 1, 0)
+        blur(0, 0)
+        blur(patches - 1, 0)
+        if step == ITERS - 1:
+            dual_store.start()
+
+        now = bar[middle, :]
+        grad_rows = jnp.where(keep_rows, bar[pl.ds(GROUP + 1, rows), :] - now, 0.0)
+        grad_cols = jnp.where(keep_cols, pltpu.roll(now, wide - 1, axis=1) - now, 0.0)
+        moved_rows = tv[0] + SIGMA * grad_rows
+        moved_cols = tv[1] + SIGMA * grad_cols
+        shrink = jnp.maximum(
+            1.0, jnp.sqrt(moved_rows * moved_rows + moved_cols * moved_cols) / TV_WEIGHT
+        )
+        new_rows = moved_rows / shrink
+        new_cols = moved_cols / shrink
+        tv[0] = new_rows
+        tv[1] = new_cols
+        masked_rows = jnp.where(keep_rows & own_lane, new_rows, 0.0)
+        masked_cols = jnp.where(keep_cols & own_lane, new_cols, 0.0)
+        total[top, :] = jnp.zeros((GROUP, wide), jnp.float32)
+        total[bottom, :] = jnp.zeros((GROUP, wide), jnp.float32)
+        total[middle, :] = pltpu.roll(masked_cols, 1, axis=1) - masked_cols - masked_rows
+        total[pl.ds(GROUP + 1, rows), :] += masked_rows
 
         def stack_dual(patch, carry):
             here = pl.ds(pl.multiple_of(patch * LANES, LANES), LANES)
@@ -263,9 +370,9 @@
 
         def put(tile, both):
             here = pl.ds(pl.multiple_of(tile * LANES, LANES), LANES)
-            total[:GROUP, here] = both[:GROUP, :LANES]
-            total[pl.ds(GROUP, rows), here] = both[GROUP:, :LANES] + both[:rows, LANES:]
-            total[pl.ds(GROUP + rows, GROUP), here] = both[rows:, LANES:]
+            total[:GROUP, here] += both[:GROUP, :LANES]
+            total[pl.ds(GROUP, rows), here] += both[GROUP:, :LANES] + both[:rows, LANES:]
+            total[pl.ds(GROUP + rows, GROUP), here] += both[rows:, LANES:]
 
         put(0, jnp.dot(stack[0], adjoint[0], preferred_element_type=jnp.float32))
 
@@ -277,38 +384,26 @@
             put(tile, both)
             return carry
 
-        lax.fori_loop(1, patches, spread, 0)
         put(
             patches,
             jnp.dot(
                 stack[patches - 1], adjoint_rest[patches - 1], preferred_element_type=jnp.float32
             ),
         )
-
-        now = bar[middle, :]
-        grad_rows = jnp.where(keep_rows, bar[pl.ds(GROUP + 1, rows), :] - now, 0.0)
-        grad_cols = jnp.where(keep_cols, pltpu.roll(now, wide - 1, axis=1) - now, 0.0)
-        moved_rows = tv[0] + SIGMA * grad_rows
-        moved_cols = tv[1] + SIGMA * grad_cols
-        shrink = jnp.maximum(
-            1.0, jnp.sqrt(moved_rows * moved_rows + moved_cols * moved_cols) / TV_WEIGHT
-        )
-        new_rows = moved_rows / shrink
-        new_cols = moved_cols / shrink
-        tv[0] = new_rows
-        tv[1] = new_cols
-        masked_rows = jnp.where(keep_rows & own_lane, new_rows, 0.0)
-        masked_cols = jnp.where(keep_cols & own_lane, new_cols, 0.0)
-        total[middle, :] += pltpu.roll(masked_cols, 1, axis=1) - masked_cols - masked_rows
-        total[pl.ds(GROUP + 1, rows), :] += masked_rows
-
+        pack(total, 0, 0, sent_cols.at[turn + 1, 0])
+        pack(total, last, half, sent_cols.at[turn + 1, 1])
         exchange = copies(turn + 1, total, sums_low, sums_high)
-        start_copies(exchange)
-        wait_copies(exchange)
+        start_copies(exchange, far)
+        lax.fori_loop(1, patches, spread, 0)
+        start_copies(exchange, near)
+        wait_copies(exchange, near + far)
 
         got = turn + 1
-        total[middle, tile_first] += got_cols[got, 0]
-        total[middle, tile_last] += got_cols[got, 1]
+        in_right = (lane >= half) & (lane < half + GROUP)
+        from_left = unpack(got_cols[got, 0], half)
+        total[middle, tile_first] += jnp.where(in_right, from_left, 0.0)
+        from_right = unpack(got_cols[got, 1], 0)
+        total[middle, tile_last] += jnp.where(lane < GROUP, from_right, 0.0)
         for side, place in ((0, pl.ds(GROUP, GROUP)), (1, pl.ds(rows, GROUP))):
             total[place, :] += got_rows[got, side]
             total[place, tile_first] += got_corners[got, 2 * side]
@@ -320,11 +415,15 @@
             image[...] = new
             following = bars.at[step + 1]
             following[middle, :] = 2.0 * new - old
+            pack(following, 0, half, sent_cols.at[turn + 2, 0])
+            pack(following, last, 0, sent_cols.at[turn + 2, 1])
             exchange = copies(turn + 2, following, image_low, image_high)
-            start_copies(exchange)
-            wait_copies(exchange)
+            start_copies(exchange, far + near)
         else:
             restored_ref[...] = pltpu.roll(new, wide - half, axis=1)[:, :cols]
+            image_store.start()
+            dual_store.wait()
+            image_store.wait()
 
 
 def per_device(observed, psf_table, psf_index, start_image, blur_dual, tv_dual):
@@ -334,21 +433,28 @@
     tiles = patches + 1
     wide = tiles * LANES
     turns = 2 * ITERS
-    whole = pl.BlockSpec(memory_space=pltpu.VMEM)
+    table = psf_table.transpose(1, 2, 0)
     deep = GROUP * LANES
     weight = pltpu.VMEM((patches, deep, 2 * LANES), jnp.bfloat16)
     f32 = jnp.float32
+    anywhere = pl.BlockSpec(memory_space=pl.ANY)
     return pl.pallas_call(
         functools.partial(body, kernel_size),
         out_shape=(
             jax.ShapeDtypeStruct((rows, cols), f32),
             jax.ShapeDtypeStruct((rows, cols), f32),
         ),
-        in_specs=[pl.BlockSpec(memory_space=pltpu.SMEM)] + [whole] * 5,
-        out_specs=(whole, whole),
+        in_specs=[pl.BlockSpec(memory_space=pltpu.SMEM)] + [anywhere] * 5,
+        out_specs=(anywhere, anywhere),
         scratch_shapes=[
-            pltpu.VMEM((patches, 2 * GROUP, LANES), f32),
-            pltpu.VMEM((patches, 2 * GROUP, LANES), f32),
+            pltpu.VMEM((rows, cols), f32),
+            pltpu.VMEM(table.shape, table.dtype),
+            pltpu.VMEM((rows, cols), f32),
+            pltpu.VMEM((2, rows, cols), f32),
+            pltpu.VMEM((rows, cols), f32),
+            pltpu.VMEM((rows, cols), f32),
+            pltpu.VMEM((2 * GROUP, 8, LANES), f32),
+            pltpu.VMEM((2 * GROUP, 8, LANES), f32),
             weight,
             weight,
             weight,
@@ -360,15 +466,17 @@
             pltpu.VMEM((rows, wide), f32),
             pltpu.VMEM((2, rows, wide), f32),
             pltpu.VMEM((turns, 2, GROUP, wide), f32),
-            pltpu.VMEM((turns, 2, rows, LANES), f32),
+            pltpu.VMEM((turns, 2, GROUP, LANES), f32),
             pltpu.VMEM((turns, 4, GROUP, LANES), f32),
+            pltpu.VMEM((turns, 2, GROUP, LANES), f32),
             pltpu.SemaphoreType.DMA((turns, 8)),
             pltpu.SemaphoreType.DMA((turns, 8)),
+            pltpu.SemaphoreType.DMA((5,)),
         ],
         compiler_params=pltpu.CompilerParams(
             collective_id=0, has_side_effects=True, vmem_limit_bytes=60 * 1024 * 1024
         ),
-    )(psf_index, observed, psf_table, start_image, blur_dual, tv_dual)
+    )(psf_index, observed, table, start_image, blur_dual, tv_dual)
 
 
 def solution(mesh):

time: 46 us -> 38.6 us (0.84)
  Pallas kernels: 39.7 us -> 35.2 us
  local copies, waits for them, and re-layouts: 4.99 us -> 2.42 us
    pallas_call x1, Pallas kernels: 39.7 us -> 35.2 us  [per_device(): pl.pallas_call(functools.partial(body, kernel_size), out_shape=(jax.Shape...]
    unnamed x5 -> x4, local copies, waits for them, and re-layouts: 4.99 us -> 2.42 us
where the time goes in v2:
time: 38.6 us; the launch traced here: 38.3 us
  Pallas kernels  35.2 us (91%)
  local copies, waits for them, and re-layouts  2.42 us (6%)
  between operations  0.65 us (2%)
    pallas_call x1, Pallas kernels, per_device(): pl.pallas_call(functools.partial(body, kernel_size), out_shape=(jax.Shape...  35.2 us
    unnamed x4, local copies, waits for them, and re-layouts  2.42 us

profile of v2, /device:TPU:11, one launch (start us, length us, event | category | flops | bytes accessed | tf_op | source)
XLA Modules:
  0.0 38.3 jit_solution(11642300450985468054)
XLA Ops:
  0.6 35.2 %shard_map.77 = (f32[128,512]{1,0:T(8,128)}, f32[128,512]{1,0:T(8,128)}) custom-call(s32[1,4]{1,0:T(1,128)} %index_ref.1, f32[128,512]{1,0:T(8,128)} %observed_hbm.1, bf16[31,31,64]{2,1,0:T(8,128)(2,1)} %bitcast.1, f32[128,512]{1,0:T(8,128)} %start_hbm.1, f32[128,512]{1,0:T(8,128)} %dual_hbm.1, f32[2,128,512]{2,1,0:T(8,128)} %tv_hbm.1), custom_call_target="tpu_custom_call" | custom-call | tf_op jit(solution)/shard_map/pallas_call | solution.py:441
  35.8 0.0 copy-start
  35.9 1.7 %copy.10 = f32[128,512]{1,0:T(8,128)} copy(f32[128,512]{1,0:T(8,128)} %get-tuple-element.4) | data formatting | bytes 524288
  37.6 0.0 copy-done
  37.6 0.7 %copy.11 = f32[128,512]{1,0:T(8,128)} copy(f32[128,512]{1,0:T(8,128)S(1)} %copy-done) | data formatting | bytes 524288
Async XLA Ops:
  35.8 1.7 %copy-start = (f32[128,512]{1,0:T(8,128)S(1)}, f32[128,512]{1,0:T(8,128)}, u32[]{:S(2)}) copy-start(f32[128,512]{1,0:T(8,128)} %get-tuple-element.5) | copy-start | bytes 786436

commit v3 on v2

--- a/solution.py
+++ b/solution.py
@@ -43,6 +43,7 @@
     adjoint,
     adjoint_rest,
     stack,
+    stack_back,
     padded_dual,
     bars,
     sums,
@@ -205,7 +206,7 @@
     pack(bars.at[0], 0, half, sent_cols.at[0, 0])
     pack(bars.at[0], last, 0, sent_cols.at[0, 1])
     exchange = copies(0, bars.at[0], image_low, image_high)
-    start_copies(exchange, far + near)
+    start_copies(exchange, near + far)
 
     padded_dual[...] = jnp.zeros_like(padded_dual)
     turned = lax.broadcasted_iota(jnp.int32, (LANES, LANES), 0)
@@ -265,7 +266,7 @@
             )
         return carry
 
-    lax.fori_loop(0, patches * GROUP, build, 0)
+    lax.fori_loop(0, patches * GROUP, build, 0, unroll=4)
 
     loads[2].wait()
     tv[0] = shifted(tv_ref[0])
@@ -334,8 +335,18 @@
             )
         stack_bar(0, 0)
         stack_bar(tiles - 1, 0)
+        def stack_dual(patch, carry):
+            here = pl.ds(pl.multiple_of(patch * LANES, LANES), LANES)
+            for shift in range(GROUP):
+                stack_back[patch, :, shift * LANES : (shift + 1) * LANES] = padded_dual[
+                    pl.ds(shift, reach), here
+                ].astype(jnp.bfloat16)
+            return carry
+
         blur(0, 0)
         blur(patches - 1, 0)
+        for patch in range(1, patches - 1):
+            stack_dual(patch, 0)
         if step == ITERS - 1:
             dual_store.start()
 
@@ -358,15 +369,8 @@
         total[middle, :] = pltpu.roll(masked_cols, 1, axis=1) - masked_cols - masked_rows
         total[pl.ds(GROUP + 1, rows), :] += masked_rows
 
-        def stack_dual(patch, carry):
-            here = pl.ds(pl.multiple_of(patch * LANES, LANES), LANES)
-            for shift in range(GROUP):
-                stack[patch, :, shift * LANES : (shift + 1) * LANES] = padded_dual[
-                    pl.ds(shift, reach), here
-                ].astype(jnp.bfloat16)
-            return carry
-
-        lax.fori_loop(0, patches, stack_dual, 0)
+        stack_dual(0, 0)
+        stack_dual(patches - 1, 0)
 
         def put(tile, both):
             here = pl.ds(pl.multiple_of(tile * LANES, LANES), LANES)
@@ -374,12 +378,12 @@
             total[pl.ds(GROUP, rows), here] += both[GROUP:, :LANES] + both[:rows, LANES:]
             total[pl.ds(GROUP + rows, GROUP), here] += both[rows:, LANES:]
 
-        put(0, jnp.dot(stack[0], adjoint[0], preferred_element_type=jnp.float32))
+        put(0, jnp.dot(stack_back[0], adjoint[0], preferred_element_type=jnp.float32))
 
         def spread(tile, carry):
-            both = jnp.dot(stack[tile], adjoint[tile], preferred_element_type=jnp.float32)
+            both = jnp.dot(stack_back[tile], adjoint[tile], preferred_element_type=jnp.float32)
             both += jnp.dot(
-                stack[tile - 1], adjoint_rest[tile - 1], preferred_element_type=jnp.float32
+                stack_back[tile - 1], adjoint_rest[tile - 1], preferred_element_type=jnp.float32
             )
             put(tile, both)
             return carry
@@ -387,7 +391,7 @@
         put(
             patches,
             jnp.dot(
-                stack[patches - 1], adjoint_rest[patches - 1], preferred_element_type=jnp.float32
+                stack_back[patches - 1], adjoint_rest[patches - 1], preferred_element_type=jnp.float32
             ),
         )
         pack(total, 0, 0, sent_cols.at[turn + 1, 0])
@@ -418,7 +422,7 @@
             pack(following, 0, half, sent_cols.at[turn + 2, 0])
             pack(following, last, 0, sent_cols.at[turn + 2, 1])
             exchange = copies(turn + 2, following, image_low, image_high)
-            start_copies(exchange, far + near)
+            start_copies(exchange, near + far)
         else:
             restored_ref[...] = pltpu.roll(new, wide - half, axis=1)[:, :cols]
             image_store.start()
@@ -460,6 +464,7 @@
             weight,
             weight,
             pltpu.VMEM((tiles, rows + GROUP, deep), jnp.bfloat16),
+            pltpu.VMEM((patches, rows + GROUP, deep), jnp.bfloat16),
             pltpu.VMEM((rows + 2 * GROUP, cols), f32),
             pltpu.VMEM((ITERS, rows + 2 * GROUP, wide), f32),
             pltpu.VMEM((ITERS, rows + 2 * GROUP, wide), f32),

time: 38.6 us -> 34.3 us (0.89)
  Pallas kernels: 35.2 us -> 30.9 us
    pallas_call x1, Pallas kernels: 35.2 us -> 30.9 us  [per_device(): pl.pallas_call(functools.partial(body, kernel_size), out_shape=(jax.Shape...]
where the time goes in v3:
time: 34.3 us; the launch traced here: 34 us
  Pallas kernels  30.9 us (90%)
  local copies, waits for them, and re-layouts  2.42 us (7%)
  between operations  0.65 us (2%)
    pallas_call x1, Pallas kernels, per_device(): pl.pallas_call(functools.partial(body, kernel_size), out_shape=(jax.Shape...  30.9 us
    unnamed x4, local copies, waits for them, and re-layouts  2.42 us

profile of v3, /device:TPU:11, one launch (start us, length us, event | category | flops | bytes accessed | tf_op | source)
XLA Modules:
  0.0 34.0 jit_solution(17712005225410087552)
XLA Ops:
  0.6 30.9 %shard_map.77 = (f32[128,512]{1,0:T(8,128)}, f32[128,512]{1,0:T(8,128)}) custom-call(s32[1,4]{1,0:T(1,128)} %index_ref.1, f32[128,512]{1,0:T(8,128)} %observed_hbm.1, bf16[31,31,64]{2,1,0:T(8,128)(2,1)} %bitcast.1, f32[128,512]{1,0:T(8,128)} %start_hbm.1, f32[128,512]{1,0:T(8,128)} %dual_hbm.1, f32[2,128,512]{2,1,0:T(8,128)} %tv_hbm.1), custom_call_target="tpu_custom_call" | custom-call | tf_op jit(solution)/shard_map/pallas_call | solution.py:445
  31.5 0.0 copy-start
  31.5 1.7 %copy.10 = f32[128,512]{1,0:T(8,128)} copy(f32[128,512]{1,0:T(8,128)} %get-tuple-element.4) | data formatting | bytes 524288
  33.2 0.0 copy-done
  33.3 0.7 %copy.11 = f32[128,512]{1,0:T(8,128)} copy(f32[128,512]{1,0:T(8,128)S(1)} %copy-done) | data formatting | bytes 524288
Async XLA Ops:
  31.5 1.7 %copy-start = (f32[128,512]{1,0:T(8,128)S(1)}, f32[128,512]{1,0:T(8,128)}, u32[]{:S(2)}) copy-start(f32[128,512]{1,0:T(8,128)} %get-tuple-element.5) | copy-start | bytes 786436
